TPU v7x, 32 devices: a whole 2x2x4 slice. The times are simulated.
32 devices in a mesh: groups: 2 (over x), wide: 8 (over z, y), narrow: 2 (over core).
Axes of the slice: x: 2, y: 2, z: 4, core: 2. Of those that a mesh axis runs over, the one named last changes fastest.
Arguments:
- tokens: bfloat16 [4096, 4096], P(('groups', 'wide')), parts along dimension 0, may hold values from -6 to 6
- norm_gain: float32 [4096], replicated, may hold values from 0.1 to 1.9
- w_in: bfloat16 [4096, 1024], P('wide'), may hold values from -0.09375 to 0.09375
- w_out: bfloat16 [1024, 4096], P('wide', 'narrow'), may hold values from -0.1875 to 0.1875
- w_up: bfloat16 [8, 1024, 2688], P('wide', None, 'narrow'), may hold values from -0.1875 to 0.1875
- w_down: bfloat16 [8, 2688, 1024], P('wide', 'narrow'), may hold values from -0.15625 to 0.15625
- expert_ids: int32 [4096, 4], P(('groups', 'wide')), parts along dimension 0, may hold values from 0 to 7, all different within a row; in each aligned block of 256 rows (0 to 255, 256 to 511, ...) at most 192 rows name the same one
- gate_weights: float32 [4096, 4], P(('groups', 'wide')), parts along dimension 0, may hold values from 0.1 to 1
Outputs:
- result: bfloat16 [4096, 4096], P(('groups', 'wide'), 'narrow'), parts along dimension 0
There are 2 independent parts, one for each index of `groups`. A program takes and returns all parts, laid end to end along the dimension named above; an argument that names none is the same for every part. Nothing has to cross between parts.
Inputs may be any that keep to these rules, and one draw needn't show every extreme that they name: `expert_ids`: within the 256 rows of one index of wide, the entries of a row differ and no expert is named by more than 192 rows.
All inputs are finite; a program needn't handle non-finite values.
Results may differ from a plain program's by a relative error of at most 0.013.
Values may be sent and summed in bfloat16 or wider, within the bound.
A program may use at most 128 MiB of HBM per device.

v0:
```python
import jax
import jax.numpy as jnp
from jax import lax
from jax.sharding import PartitionSpec as P


def local(tokens, norm_gain, w_in, w_out, w_up, w_down, expert_ids, gate_weights):
    experts = lax.axis_size("wide")
    tok_rows = tokens.shape[0]
    top_count = expert_ids.shape[1]
    capacity = 3 * tok_rows * top_count // (2 * experts)
    full_in, full_out = (
        lax.all_gather(w_in, "wide", axis=0, tiled=True),
        lax.all_gather(w_out, "wide", axis=0, tiled=True),
    )
    widened = tokens.astype(jnp.float32)
    scale = lax.rsqrt(jnp.mean(widened * widened, axis=-1, keepdims=True) + 1e-05)
    normed = (widened * scale * norm_gain).astype(jnp.bfloat16)
    latent = jnp.dot(normed, full_in, preferred_element_type=jnp.float32).astype(jnp.bfloat16)
    width = latent.shape[1]
    flat_ids = expert_ids.reshape(-1)
    onehot = (flat_ids[:, None] == jnp.arange(experts, dtype=jnp.int32)[None, :]).astype(jnp.int32)
    slot_index = jnp.sum((jnp.cumsum(onehot, axis=0) - 1) * onehot, axis=-1)
    target = flat_ids * capacity + slot_index
    repeated = jnp.repeat(latent, top_count, axis=0)
    buffer = jnp.zeros((experts * capacity, width), jnp.bfloat16).at[target].set(repeated)
    buffer = buffer.reshape(experts, capacity, width)
    up_weight = w_up[0]
    down_weight = w_down[0]
    received = lax.all_to_all(buffer, "wide", split_axis=0, concat_axis=0, tiled=True)
    sources = received.shape[0]
    items = received.shape[1]
    rows = received.reshape(sources * items, received.shape[2])
    hidden = jnp.dot(rows, up_weight, preferred_element_type=jnp.float32)
    hidden = jnp.square(jnp.maximum(hidden, 0.0)).astype(jnp.bfloat16)
    partial_value = jnp.dot(hidden, down_weight, preferred_element_type=jnp.float32)
    summed = lax.psum_scatter(
        partial_value.astype(jnp.bfloat16), "narrow", scatter_dimension=1, tiled=True
    ).astype(jnp.float32)
    outgoing = summed.astype(jnp.bfloat16).reshape(sources, items, summed.shape[1])
    returned = lax.all_to_all(outgoing, "wide", split_axis=0, concat_axis=0, tiled=True)
    columns = returned.shape[2]
    flat_back = returned.reshape(experts * capacity, columns)
    picked = flat_back[target].astype(jnp.float32).reshape(tok_rows, top_count, columns)
    mixture = jnp.sum(picked * gate_weights[:, :, None], axis=1).astype(jnp.bfloat16)
    mixture = lax.all_gather(mixture, "narrow", axis=1, tiled=True)
    branch = jnp.dot(mixture, full_out, preferred_element_type=jnp.float32)
    half_width = full_out.shape[1]
    own_half = lax.dynamic_slice_in_dim(
        widened, lax.axis_index("narrow") * half_width, half_width, 1
    )
    return (own_half + branch).astype(jnp.bfloat16)


def solution(mesh):
    in_specs = (
        P(("groups", "wide"), None),
        P(),
        P("wide", None),
        P("wide", "narrow"),
        P("wide", None, "narrow"),
        P("wide", "narrow", None),
        P(("groups", "wide"), None),
        P(("groups", "wide"), None),
    )
    out_specs = P(("groups", "wide"), "narrow")
    return jax.shard_map(local, mesh=mesh, in_specs=in_specs, out_specs=out_specs, check_vma=False)
```

profile of v0, /device:TPU:20, one launch (start us, length us, event | category | flops | bytes accessed | tf_op | source)
XLA Modules:
  0.0 360.2 jit_solution(6078926013426687952)
XLA Ops:
  6.5 0.7 all-gather.3.cloned.1.call-update
  7.3 0.9 copy.11
  8.5 2.3 reduce-window.6
  11.2 0.7 broadcast_multiply_fusion
  12.2 2.1 multiply_reduce_fusion
  14.4 118.8 %all-gather.3.cloned.1.call-done = bf16[4096,1024]{1,0:T(8,128)(2,1)} async-done(((bf16[512,1024]{1,0:T(8,128)(2,1)}), bf16[4096,1024]{1,0:T(8,128)(2,1)}) %all-gather.3.cloned.1.call-update) | async-done | bytes 8388624 | tf_op jit(solution)/shard_map/all_gather | solution.py:13
  133.2 6.4 %fusion.11 = bf16[256,1024]{1,0:T(8,128)(2,1)S(1)} fusion(bf16[4096,1024]{1,0:T(8,128)(2,1)} %all-gather.3.cloned.1.call-done, f32[4096]{0:T(1024)S(1)} %copy-done.3, f32[256]{0:T(256)S(1)} %add_rsqrt_fusion, bf16[256,4096]{1,0:T(8,128)(2,1)} %param.8), kind=kOutput, calls=%fused_computation.19 | convolution fusion | flops 2151940096 | bytes 11027456 | tf_op jit(solution)/shard_map/dot_general | solution.py:19
  139.6 2.0 broadcast_in_dim.5
  141.6 4.0 %reshape.96 = bf16[1024,1024]{1,0:T(8,128)(2,1)} reshape(bf16[256,4,1024]{2,1,0:T(4,128)(2,1)} %broadcast_in_dim.5) | data formatting | bytes 4194304 | tf_op jit(solution)/shard_map/reshape | solution.py:25
  145.5 8.1 %scatter_custom_fusion = bf16[1536,1024]{1,0:T(8,128)(2,1)} fusion(s32[1024]{0:T(1024)S(1)} %bitcast.36, bf16[1024,1024]{1,0:T(8,128)(2,1)} %reshape.96, bf16[]{:T(256)} %constant.6.clone.1), kind=kCustom, calls=%fused_computation.17 | custom fusion | bytes 3146240 | tf_op jit(solution)/shard_map/scatter | solution.py:26
  153.6 73.0 %all_to_all.10 = bf16[8,192,1024]{2,1,0:T(8,128)(2,1)S(1)} all-to-all(bf16[8,192,1024]{2,1,0:T(8,128)(2,1)} %bitcast.32), channel_id=1, replica_groups=mesh['groups'=2,'wide'=8,'narrow'=2] {'wide'}, dimensions={0} | all-to-all | bytes 6291456 | tf_op jit(solution)/shard_map/all_to_all | solution.py:30
  226.6 5.3 %fusion.1 = bf16[1536,1344]{1,0:T(8,128)(2,1)S(1)} fusion(bf16[1536,1024]{1,0:T(8,128)(2,1)S(1)} %bitcast.33, bf16[1,1024,1344]{1,2,0:T(8,128)(2,1)S(1)} %copy-done), kind=kOutput, calls=%fused_computation.4 | convolution fusion | flops 4234051584 | bytes 10027008 | tf_op jit(solution)/shard_map/dot_general | solution.py:34
  232.0 6.4 %convolution_convert_fusion = bf16[1536,1024]{1,0:T(8,128)(2,1)} fusion(bf16[1536,1344]{1,0:T(8,128)(2,1)S(1)} %fusion.1, bf16[1,1344,1024]{2,1,0:T(8,128)(2,1)S(1)} %copy-done.2), kind=kOutput, calls=%fused_computation.7 | convolution fusion | flops 4229431296 | bytes 10027008 | tf_op jit(solution)/shard_map/dot_general | solution.py:36
  238.4 0.7 all-gather.5.cloned.1.call-update
  239.1 12.3 %reduce-scatter.2.cloned.1.call-done = bf16[1536,512]{1,0:T(8,128)(2,1)} async-done(((bf16[1536,1024]{1,0:T(8,128)(2,1)}), bf16[1536,512]{1,0:T(8,128)(2,1)}) %reduce-scatter.2.cloned.1.call-update) | async-done | bytes 1572880 | tf_op jit(solution)/shard_map/reduce_scatter | solution.py:37
  251.5 6.2 %all-to-all-start.1 = ((bf16[8,192,512]{2,1,0:T(8,128)(2,1)}), bf16[8,192,512]{2,1,0:T(8,128)(2,1)}, u32[]{:S(2)}, u32[]{:S(2)}) async-start(bf16[8,192,512]{2,1,0:T(8,128)(2,1)} %bitcast.34), calls=%async_computation.2 | async-start | bytes 3145728 | tf_op jit(solution)/shard_map/all_to_all | solution.py:41
  257.7 4.1 %convert_element_type.35 = f32[256,4096]{1,0:T(8,128)} convert(bf16[256,4096]{1,0:T(8,128)(2,1)} %param.8) | non-fusion elementwise | flops 1048576 | bytes 6291456 | tf_op jit(solution)/shard_map/convert_element_type | solution.py:16
  261.9 46.6 %all-to-all-done.1 = bf16[8,192,512]{2,1,0:T(8,128)(2,1)} async-done(((bf16[8,192,512]{2,1,0:T(8,128)(2,1)}), bf16[8,192,512]{2,1,0:T(8,128)(2,1)}, u32[]{:S(2)}, u32[]{:S(2)}) %all-to-all-start.1) | async-done | bytes 1572896 | tf_op jit(solution)/shard_map/all_to_all | solution.py:41
  308.5 6.7 %gather_fusion = bf16[1024,512]{1,0:T(8,128)(2,1)} fusion(bf16[1536,512]{1,0:T(8,128)(2,1)} %bitcast.8, s32[1024]{0:T(1024)S(1)} %broadcast_clamp_fusion), kind=kCustom, calls=%fused_computation | custom fusion | bytes 2101248 | tf_op jit(solution)/shard_map/gather | solution.py:44
  315.2 2.8 reshape.83
  318.0 3.0 multiply_reduce_fusion.1
  321.0 2.2 all_gather.10
  323.2 25.4 %all-gather.5.cloned.1.call-done = bf16[1024,2048]{1,0:T(8,128)(2,1)} async-done(((bf16[128,2048]{1,0:T(8,128)(2,1)}), bf16[1024,2048]{1,0:T(8,128)(2,1)}) %all-gather.5.cloned.1.call-update) | async-done | bytes 4194320 | tf_op jit(solution)/shard_map/all_gather | solution.py:14
  348.6 5.1 %fusion.4 = bf16[256,2048]{1,0:T(8,128)(2,1)} fusion(bf16[256,1024]{1,0:T(8,128)(2,1)S(1)} %all_gather.10, bf16[1024,2048]{1,0:T(8,128)(2,1)} %all-gather.5.cloned.1.call-done, f32[256,4096]{1,0:T(8,128)} %convert_element_type.35, s32[]{:T(128)S(6)} %select_n.14), kind=kOutput, calls=%fused_computation.11 | convolution fusion | flops 1074790400 | bytes 7864324 | tf_op jit(solution)/shard_map/dot_general | solution.py:47
  (25 shorter events, 1.3 us)
Async XLA Ops:
  6.5 220.1 %copy-start = (bf16[1,1024,1344]{1,2,0:T(8,128)(2,1)S(1)}, bf16[1,1024,1344]{1,2,0:T(8,128)(2,1)}, u32[]{:S(2)}) copy-start(bf16[1,1024,1344]{1,2,0:T(8,128)(2,1)} %param.12) | copy-start | bytes 8257540
  6.5 126.6 %copy-start.3 = (f32[4096]{0:T(1024)S(1)}, f32[4096]{0:T(1024)}, u32[]{:S(2)}) copy-start(f32[4096]{0:T(1024)} %param.9) | copy-start | bytes 49156
  6.5 126.6 %all-gather.3.cloned.1.call-start = ((), (), s32[]{:S(2)}) async-start(), calls=%async_computation.3 | async-start | bytes 9437184 | tf_op jit(solution)/shard_map/all_gather | solution.py:13
  7.3 244.2 %reduce-scatter.2.cloned.1.call-start = ((), (), s32[]{:S(2)}) async-start(), calls=%async_computation.4 | async-start | bytes 4718592 | tf_op jit(solution)/shard_map/reduce_scatter | solution.py:37
  226.6 5.3 %copy-start.2 = (bf16[1,1344,1024]{2,1,0:T(8,128)(2,1)S(1)}, bf16[1,1344,1024]{2,1,0:T(8,128)(2,1)}, u32[]{:S(2)}) copy-start(bf16[1,1344,1024]{2,1,0:T(8,128)(2,1)} %param.13) | copy-start | bytes 8257540
  238.4 110.2 %all-gather.5.cloned.1.call-start = ((), (), s32[]{:S(2)}) async-start(), calls=%async_computation.5 | async-start | bytes 4718592 | tf_op jit(solution)/shard_map/all_gather | solution.py:14
  251.5 57.1 %all-to-all-start.1 = ((bf16[8,192,512]{2,1,0:T(8,128)(2,1)}), bf16[8,192,512]{2,1,0:T(8,128)(2,1)}, u32[]{:S(2)}, u32[]{:S(2)}) async-start(bf16[8,192,512]{2,1,0:T(8,128)(2,1)} %bitcast.34), calls=%async_computation.2 | async-start | bytes 3145728 | tf_op jit(solution)/shard_map/all_to_all | solution.py:41
  257.7 4.1 %copy-start.1 = (f32[256,4]{0,1:T(4,128)S(1)}, f32[256,4]{0,1:T(4,128)}, u32[]{:S(2)}) copy-start(f32[256,4]{0,1:T(4,128)} %param.15) | copy-start | bytes 12292
Sparse Core Ops, SparseCore 0:
  9.5 123.6 all-gather.2
  238.5 12.9 reduce-scatter.1
  253.6 94.9 all-gather.4
where the time goes:
time: 364 us; the launch traced here: 360 us
  waiting for transfers between devices  205 us (56%)
  blocking collectives  75.2 us (21%)
  local copies, waits for them, and re-layouts  25.3 us (7%)
  matrix products  23.2 us (6%)
  between operations  13.2 us (4%)
  other arithmetic  12.4 us (3%)
  starting transfers between devices  6.29 us (2%)
    all_gather x1, waiting for transfers between devices, local(): lax.all_gather(w_in, 'wide', axis=0, tiled=True)  119 us
    all_to_all x1, blocking collectives, local(): lax.all_to_all(buffer, 'wide', split_axis=0, concat_axis=0, tiled=True)  73 us
    all_to_all x1, waiting for transfers between devices, local(): lax.all_to_all(outgoing, 'wide', split_axis=0, concat_axis=0, tiled=True)  46.6 us
    all_gather x1, waiting for transfers between devices, local(): lax.all_gather(w_out, 'wide', axis=0, tiled=True)  25.4 us
    reduce_scatter x1, waiting for transfers between devices, local(): lax.psum_scatter(partial_value.astype(jnp.bfloat16), 'narrow', scatter_di...  12.3 us
    scatter x1, local copies, waits for them, and re-layouts, local(): jnp.zeros((experts * capacity, width), jnp.bfloat16).at[target]  8.06 us
  transfers between devices with their start and end apart: 4, of which 4 were waited for; matrix products, arithmetic and copies ran while one was open for 7% of the time, Pallas kernels for 0%

commit v1 on v0

v1 whole, which is shorter than its diff:
```python
import functools
import jax
import jax.numpy as jnp
from jax import lax
from jax.experimental import pallas as pl
from jax.experimental.pallas import tpu as pltpu
from jax.sharding import PartitionSpec as P

F32 = jnp.float32
BF16 = jnp.bfloat16


def kernel(
    tok_hbm, gain_ref, win_hbm, wout_hbm, up_hbm, down_hbm, gates_hbm, out_ref,
    tok, nb, win, wo, up, down, gbuf, lat, acc, xsend, obuf, ownp, ysend, yrecv, zsend, zrecv, macc, mixb,
    loc, gs, gr, es, er, az_s, az_r, ay_s, ay_r, ax_s, ax_r, bz_s, bz_r, by_s, by_r, bx_s, bx_r,
    cz_s, cz_r, cy_s, cy_r, cc_s, cc_r, dy_s, dy_r, dz_s, dz_r, mc_s, mc_r,
):
    wide = lax.axis_size("wide")
    zs = wide // 2
    g, w, c = lax.axis_index("groups"), lax.axis_index("wide"), lax.axis_index("narrow")
    z, y = w // 2, w % 2
    gh = g % 2
    xpeer = {"groups": g + 1 - 2 * gh}
    ypeer = {"wide": w + 1 - 2 * y}
    cpeer = {"narrow": 1 - c}
    MESH = pl.DeviceIdType.MESH

    def zfwd(k):
        return {"wide": lax.rem(z + k, zs) * 2 + y}

    def zback(k):
        return {"wide": lax.rem(z + zs - k, zs) * 2 + y}

    def blk(k, yy):
        return lax.rem(z + zs - k, zs) * 2 + yy

    def rcopy(src, dst, ss, rs, dev):
        return pltpu.make_async_remote_copy(
            src_ref=src, dst_ref=dst, send_sem=ss, recv_sem=rs, device_id=dev, device_id_type=MESH
        )

    def loop(lo, hi, body):
        def step(i, carry):
            body(i)
            return carry

        lax.fori_loop(lo, hi, step, 0)

    half_in = win.shape[2]
    lcols = win.shape[3]
    half_out = wo.shape[2]
    tokens = tok.shape[0]
    th = lat.shape[2]
    oy = 1 - y

    in_cols = pl.ds(pl.multiple_of(c * lcols, lcols), lcols)
    lc_tok = pltpu.make_async_copy(tok_hbm, tok, loc.at[0])
    lc_in = [
        pltpu.make_async_copy(
            win_hbm.at[pl.ds(h * half_in, half_in), in_cols], win.at[w, h], loc.at[1 + h]
        )
        for h in range(2)
    ]
    lc_out = [
        pltpu.make_async_copy(wout_hbm.at[pl.ds(h * half_out, half_out), :], wo.at[w, h], loc.at[3 + h])
        for h in range(2)
    ]
    lc_up = pltpu.make_async_copy(up_hbm.at[0], up.at[c], loc.at[5])
    lc_down = pltpu.make_async_copy(down_hbm.at[0], down.at[c], loc.at[6])
    lc_g = pltpu.make_async_copy(gates_hbm.at[c], gbuf.at[w], loc.at[7])
    for cp in lc_in + [lc_tok, lc_g, lc_up, lc_down] + lc_out:
        cp.start()

    barrier = pltpu.get_barrier_semaphore()
    loop(1, wide, lambda d: pl.semaphore_signal(
        barrier, inc=1, device_id={"wide": lax.rem(w + d, wide)}, device_id_type=MESH))
    pl.semaphore_signal(barrier, inc=1, device_id=xpeer, device_id_type=MESH)
    pl.semaphore_signal(barrier, inc=1, device_id=cpeer, device_id_type=MESH)
    pl.semaphore_wait(barrier, wide + 1)

    def gather(buf, z_s, z_r, y_s, y_r, x_s, x_r):
        def zc(k):
            return rcopy(buf.at[w, gh], buf.at[w, gh], z_s.at[k], z_r.at[k], zfwd(k))

        def zw(k):
            s = buf.at[blk(k, y), gh]
            return rcopy(s, s, z_s.at[k], z_r.at[k], zfwd(k))

        def yc(k):
            s = buf.at[blk(k, y), gh]
            return rcopy(s, s, y_s.at[k], y_r.at[k], ypeer)

        def yw(k):
            s = buf.at[blk(k, oy), gh]
            return rcopy(s, s, y_s.at[k], y_r.at[k], ypeer)

        def x_copy(k, far):
            s = buf.at[blk(k, oy if far else y), gh]
            i = k + zs if far else k
            return rcopy(s, s, x_s.at[i], x_r.at[i], xpeer)

        def x_wait(k, far):
            s = buf.at[blk(k, oy if far else y), 1 - gh]
            i = k + zs if far else k
            return rcopy(s, s, x_s.at[i], x_r.at[i], xpeer)

        return zc, zw, yc, yw, x_copy, x_wait

    azc, azw, ayc, ayw, axc, axw = gather(win, az_s, az_r, ay_s, ay_r, ax_s, ax_r)
    bzc, bzw, byc, byw, bxc, bxw = gather(wo, bz_s, bz_r, by_s, by_r, bx_s, bx_r)

    lc_in[0].wait()
    lc_in[1].wait()
    loop(1, zs, lambda k: azc(k).start())
    ayc(0).start()

    e_up = rcopy(up_hbm.at[0], up.at[c], es.at[0], er.at[0], cpeer)
    e_down = rcopy(down_hbm.at[0], down.at[c], es.at[1], er.at[1], cpeer)
    e_up.start()
    e_down.start()
    lc_g.wait()

    def gcopy(d):
        return rcopy(gbuf.at[w], gbuf.at[w], gs.at[d], gr.at[d], {"wide": lax.rem(w + d, wide)})

    def gwait(d):
        s = gbuf.at[lax.rem(w + wide - d, wide)]
        return rcopy(s, s, gs.at[d], gr.at[d], {"wide": lax.rem(w + d, wide)})

    loop(1, wide, lambda d: gcopy(d).start())

    lc_tok.wait()
    step_rows = 32
    rin = nb.shape[2]

    def norm(i):
        rows = pl.ds(pl.multiple_of(i * step_rows, step_rows), step_rows)
        x = tok[rows, :].astype(F32)
        scale = lax.rsqrt(jnp.mean(x * x, axis=-1, keepdims=True) + 1e-05)
        n = (x * scale * gain_ref[...]).astype(BF16)
        for j in range(wide):
            nb[j, rows, :] = n[:, j * rin : (j + 1) * rin]

    loop(0, tokens // step_rows, norm)

    def madd(b):
        wb = win[b].reshape(2 * half_in, lcols)
        acc[...] += jnp.dot(nb[b], wb, preferred_element_type=F32)

    acc[...] = jnp.zeros_like(acc)
    madd(w)

    def z_arrive(k):
        azw(k).wait_recv()
        axc(k, False).start()
        ayc(k).start()

    ayw(0).wait_recv()
    axc(0, True).start()
    loop(1, zs, z_arrive)

    def y_arrive(k):
        ayw(k).wait_recv()
        axc(k, True).start()

    loop(1, zs, y_arrive)
    lc_out[0].wait()
    lc_out[1].wait()
    loop(1, zs, lambda k: bzc(k).start())

    def use_far(k):
        axw(k, True).wait_recv()
        madd(blk(k, oy))

    def use_near(k):
        axw(k, False).wait_recv()
        madd(blk(k, y))

    use_far(0)
    loop(1, zs, use_near)
    loop(1, zs, use_far)

    lat[w, c] = acc[pl.ds(pl.multiple_of(c * th, th), th), :].astype(BF16)
    xsend[...] = acc[pl.ds(pl.multiple_of((1 - c) * th, th), th), :].astype(BF16)
    swap = rcopy(xsend, lat.at[w, c], cc_s, cc_r, cpeer)
    swap.start()
    rcopy(xsend, lat.at[w, 1 - c], cc_s, cc_r, cpeer).wait_recv()

    def czc(k):
        return rcopy(lat.at[w], lat.at[w], cz_s.at[k], cz_r.at[k], zfwd(k))

    def czw(k):
        s = lat.at[blk(k, y)]
        return rcopy(s, s, cz_s.at[k], cz_r.at[k], zfwd(k))

    def cyc(k):
        s = lat.at[blk(k, y)]
        return rcopy(s, s, cy_s.at[k], cy_r.at[k], ypeer)

    def cyw(k):
        s = lat.at[blk(k, oy)]
        return rcopy(s, s, cy_s.at[k], cy_r.at[k], ypeer)

    cyc(0).start()
    loop(1, zs, lambda k: czc(k).start())

    lc_up.wait()
    lc_down.wait()
    rcopy(up_hbm.at[0], up.at[1 - c], es.at[0], er.at[0], cpeer).wait_recv()
    rcopy(down_hbm.at[0], down.at[1 - c], es.at[1], er.at[1], cpeer).wait_recv()
    loop(1, wide, lambda d: gwait(d).wait_recv())

    def gate_col(b):
        gt = gbuf[b]
        mine = lax.broadcasted_iota(jnp.int32, gt.shape, 0) == w
        row = jnp.sum(jnp.where(mine, gt, 0.0), axis=0, keepdims=True)
        return jnp.transpose(jnp.broadcast_to(row, (8, th)))[:, :1]

    def dyc(k):
        return rcopy(ysend.at[k], yrecv.at[k], dy_s.at[k], dy_r.at[k], ypeer)

    def dzc(k):
        return rcopy(zsend.at[k], zrecv.at[k], dz_s.at[k], dz_r.at[k], zback(k))

    def expert(k):
        b0 = blk(k, 0)
        x0 = jnp.concatenate([lat[b0, 0], lat[b0 + 1, 0]], axis=0)
        x1 = jnp.concatenate([lat[b0, 1], lat[b0 + 1, 1]], axis=0)
        x = jnp.concatenate([x0, x1], axis=1)
        total = None
        for h in range(2):
            hid = jnp.dot(x, up[h], preferred_element_type=F32)
            hid = jnp.square(jnp.maximum(hid, 0.0)).astype(BF16)
            part = jnp.dot(hid, down[h], preferred_element_type=F32)
            total = part if total is None else total + part
        obuf[0] = total[:th] * gate_col(b0)
        obuf[1] = total[th:] * gate_col(b0 + 1)
        ysend[k] = obuf[oy].astype(BF16)
        dyc(k).start()
        ownp[lax.rem(k, 2)] = obuf[y]

    def finish(k):
        dyc(k).wait_recv()
        zsend[k] = (ownp[lax.rem(k, 2)] + yrecv[k].astype(F32)).astype(BF16)
        dzc(k).start()

    def arrive(k):
        czw(k).wait_recv()
        cyc(k).start()

    loop(1, zs, arrive)
    cyw(0).wait_recv()
    expert(0)

    def b_arrive(k):
        bzw(k).wait_recv()
        bxc(k, False).start()

    loop(1, zs, b_arrive)

    def expert_step(k):
        cyw(k).wait_recv()
        expert(k)

        @pl.when(k > 1)
        def _():
            finish(k - 1)

        @pl.when(k == 1)
        def _():
            dyc(0).wait_recv()
            macc[...] = ownp[0] + yrecv[0].astype(F32)

    loop(1, zs, expert_step)
    loop(0, zs, lambda k: byc(k).start())
    finish(zs - 1)

    def by_arrive(k):
        byw(k).wait_recv()
        bxc(k, True).start()

    loop(0, zs, by_arrive)

    def collect(k):
        dzc(k).wait_recv()
        macc[...] += zrecv[k].astype(F32)

    loop(1, zs, collect)
    mixb[c] = macc[...].astype(BF16)
    mcopy = rcopy(mixb.at[c], mixb.at[c], mc_s, mc_r, cpeer)
    mcopy.start()
    rcopy(mixb.at[1 - c], mixb.at[1 - c], mc_s, mc_r, cpeer).wait_recv()
    loop(1, zs, lambda k: bxw(k, False).wait_recv())
    loop(0, zs, lambda k: bxw(k, True).wait_recv())

    ocols = out_ref.shape[1]
    width = min(512, ocols)

    def project(i):
        m = mixb[...].reshape(tokens, mixb.shape[2])
        off = pl.multiple_of(i * width, width)
        wv = wo[:, :, :, pl.ds(off, width)].reshape(mixb.shape[2], width)
        branch = jnp.dot(m, wv, preferred_element_type=F32)
        own = tok[:, pl.ds(pl.multiple_of(c * ocols + off, width), width)].astype(F32)
        out_ref[:, pl.ds(off, width)] = (own + branch).astype(out_ref.dtype)

    loop(0, ocols // width, project)

    loop(1, wide, lambda d: gcopy(d).wait_send())
    e_up.wait_send()
    e_down.wait_send()
    swap.wait_send()
    mcopy.wait_send()
    for zc, yc, xc in ((azc, ayc, axc), (bzc, byc, bxc)):
        loop(1, zs, lambda k: zc(k).wait_send())
        loop(0, zs, lambda k: yc(k).wait_send())
        loop(1, zs, lambda k: xc(k, False).wait_send())
        loop(0, zs, lambda k: xc(k, True).wait_send())
    loop(1, zs, lambda k: czc(k).wait_send())
    loop(0, zs, lambda k: cyc(k).wait_send())
    loop(0, zs, lambda k: dyc(k).wait_send())
    loop(1, zs, lambda k: dzc(k).wait_send())


def local(tokens, norm_gain, w_in, w_out, w_up, w_down, expert_ids, gate_weights):
    wide = lax.axis_size("wide")
    zs = wide // 2
    rows, depth = tokens.shape
    half = rows // 2
    latent = w_in.shape[1]
    ids = expert_ids.T
    chosen = ids[:, None, :] == jnp.arange(wide, dtype=jnp.int32)[None, :, None]
    gates = jnp.sum(jnp.where(chosen, gate_weights.T[:, None, :], 0.0), axis=0)
    gates = gates.reshape(wide, 2, half).transpose(1, 0, 2)
    any_ = pl.BlockSpec(memory_space=pl.ANY)
    vmem = pl.BlockSpec(memory_space=pltpu.VMEM)
    dma = pltpu.SemaphoreType.DMA
    hid = w_up.shape[2]
    cols = w_out.shape[1]
    V = pltpu.VMEM
    scratch = [
        V((rows, depth), BF16),
        V((wide, rows, depth // wide), BF16),
        V((wide, 2, w_in.shape[0] // 2, latent // 2), BF16),
        V((wide, 2, w_out.shape[0] // 2, cols), BF16),
        V((2, latent, hid), BF16),
        V((2, hid, latent), BF16),
        V((wide, wide, half), F32),
        V((wide, 2, half, latent // 2), BF16),
        V((rows, latent // 2), F32),
        V((half, latent // 2), BF16),
        V((2, half, latent), F32),
        V((2, half, latent), F32),
        V((zs, half, latent), BF16),
        V((zs, half, latent), BF16),
        V((zs, half, latent), BF16),
        V((zs, half, latent), BF16),
        V((half, latent), F32),
        V((2, half, latent), BF16),
        dma((8,)),
        dma((wide,)), dma((wide,)),
        dma((2,)), dma((2,)),
    ]
    scratch += [dma((zs,)), dma((zs,)), dma((zs,)), dma((zs,)), dma((wide,)), dma((wide,))] * 2
    scratch += [dma((zs,))] * 4 + [dma, dma] + [dma((zs,))] * 4 + [dma, dma]
    return pl.pallas_call(
        kernel,
        out_shape=jax.ShapeDtypeStruct((rows, cols), BF16),
        in_specs=[any_, vmem, any_, any_, any_, any_, any_],
        out_specs=vmem,
        scratch_shapes=scratch,
        compiler_params=pltpu.CompilerParams(
            collective_id=0, has_side_effects=True, vmem_limit_bytes=66_000_000
        ),
        name="moe",
    )(tokens, norm_gain.reshape(1, depth), w_in, w_out, w_up, w_down, gates)


def solution(mesh):
    in_specs = (
        P(("groups", "wide"), None),
        P(),
        P("wide", None),
        P("wide", "narrow"),
        P("wide", None, "narrow"),
        P("wide", "narrow", None),
        P(("groups", "wide"), None),
        P(("groups", "wide"), None),
    )
    out_specs = P(("groups", "wide"), "narrow")
    return jax.shard_map(local, mesh=mesh, in_specs=in_specs, out_specs=out_specs, check_vma=False)
```

time: 364 us -> 158 us (0.43)
  waiting for transfers between devices: 205 us -> 0 us
  Pallas kernels: 0 us -> 149 us
  blocking collectives: 75.2 us -> 0 us
  matrix products: 23.2 us -> 0 us
  local copies, waits for them, and re-layouts: 25.3 us -> 6.83 us
  between operations: 13.2 us -> 0.01 us
  other arithmetic: 12.4 us -> 1.31 us
  starting transfers between devices: 6.29 us -> 0 us
    pallas_call x0 -> x1, Pallas kernels: none -> 149 us  [local(): pl.pallas_call(kernel, out_shape=jax.ShapeDtypeStruct((rows, cols), BF16)...]
    all_gather x2 -> x0, waiting for transfers between devices: 144 us -> none  [the longest x1 119 us: local(): lax.all_gather(w_in, 'wide', axis=0, tiled=True)]
    all_to_all x1 -> x0, blocking collectives: 73 us -> none  [local(): lax.all_to_all(buffer, 'wide', split_axis=0, concat_axis=0, tiled=True)]
    all_to_all x1 -> x0, waiting for transfers between devices: 46.6 us -> none  [local(): lax.all_to_all(outgoing, 'wide', split_axis=0, concat_axis=0, tiled=True)]
    dot_general x4 -> x0, matrix products: 23.2 us -> none  [the longest x1 6.41 us: local(): jnp.dot(hidden, down_weight, preferred_element_type=jnp.float32)]
    reduce_scatter x1 -> x0, waiting for transfers between devices: 12.3 us -> none  [local(): lax.psum_scatter(partial_value.astype(jnp.bfloat16), 'narrow', scatter_di...]
    scatter x1 -> x0, local copies, waits for them, and re-layouts: 8.06 us -> none  [local(): jnp.zeros((experts * capacity, width), jnp.bfloat16).at[target]]
    gather x1 -> x0, local copies, waits for them, and re-layouts: 6.73 us -> none  [local(): flat_back[target].astype(jnp.float32).reshape(tok_rows, top_count, columns)]
  transfers between devices with their start and end apart: 4 -> 0, of which waited for: 4 -> 0; matrix products, arithmetic and copies ran while one was open for 7% -> 0% of each run, Pallas kernels for 0% -> 0%
where the time goes in v1:
time: 158 us; the launch traced here: 157 us
  Pallas kernels  149 us (94%)
  local copies, waits for them, and re-layouts  6.83 us (4%)
    pallas_call x1, Pallas kernels, local(): pl.pallas_call(kernel, out_shape=jax.ShapeDtypeStruct((rows, cols), BF16)...  149 us
    unnamed x2, local copies, waits for them, and re-layouts  6.83 us

profile of v1, /device:TPU:20, one launch (start us, length us, event | category | flops | bytes accessed | tf_op | source)
XLA Modules:
  0.0 156.7 jit_solution(909920866797237319)
XLA Ops:
  0.0 1.3 select_reduce_fusion
  1.3 4.5 %copy.10.up_hbm = bf16[1,1024,1344]{2,1,0:T(8,128)(2,1)} copy(bf16[1,1024,1344]{1,2,0:T(8,128)(2,1)} %param.12) | data formatting | bytes 5505024 | tf_op args[4]
  5.8 148.6 %moe.1 = bf16[256,2048]{1,0:T(8,128)(2,1)} custom-call(bf16[256,4096]{1,0:T(8,128)(2,1)} %tok_hbm.1, f32[1,4096]{1,0:T(1,128)} %bitcast.7, bf16[512,1024]{1,0:T(8,128)(2,1)} %win_hbm.1, bf16[128,2048]{1,0:T(8,128)(2,1)} %wout_hbm.1, bf16[1,1024,1344]{2,1,0:T(8,128)(2,1)} %copy.10.up_hbm, bf16[1,1344,1024]{2,1,0:T(8,128)(2,1)} %down_hbm.1, f32[2,8,128]{2,1,0:T(8,128)} %bitcast.6), custom_call_target="tpu_custom_call" | custom-call | tf_op jit(solution)/shard_map/moe/pallas_call | solution.py:367
  154.4 2.3 %copy.12 = bf16[256,2048]{1,0:T(8,128)(2,1)} copy(bf16[256,2048]{1,0:T(8,128)(2,1)} %moe.1) | data formatting | bytes 2097152

commit v2 on v1

--- a/solution.py
+++ b/solution.py
@@ -12,8 +12,8 @@
 
 def kernel(
     tok_hbm, gain_ref, win_hbm, wout_hbm, up_hbm, down_hbm, gates_hbm, out_ref,
-    tok, nb, win, wo, up, down, gbuf, lat, acc, xsend, obuf, ownp, ysend, yrecv, zsend, zrecv, macc, mixb,
-    loc, gs, gr, es, er, az_s, az_r, ay_s, ay_r, ax_s, ax_r, bz_s, bz_r, by_s, by_r, bx_s, bx_r,
+    tok, nb, nby, win, wo, up, down, gbuf, lat, acc, psend, precv, xsend, obuf, ownp, ysend, yrecv, zsend, zrecv, macc, mixb,
+    loc, gs, gr, es, er, az_s, az_r, ax_s, ax_r, ty_s, ty_r, tc_s, tc_r, py_s, py_r, bz_s, bz_r, by_s, by_r, bx_s, bx_r,
     cz_s, cz_r, cy_s, cy_r, cc_s, cc_r, dy_s, dy_r, dz_s, dz_r, mc_s, mc_r,
 ):
     wide = lax.axis_size("wide")
@@ -58,7 +58,7 @@
     lc_tok = pltpu.make_async_copy(tok_hbm, tok, loc.at[0])
     lc_in = [
         pltpu.make_async_copy(
-            win_hbm.at[pl.ds(h * half_in, half_in), in_cols], win.at[w, h], loc.at[1 + h]
+            win_hbm.at[pl.ds(h * half_in, half_in), in_cols], win.at[z, h], loc.at[1 + h]
         )
         for h in range(2)
     ]
@@ -107,13 +107,29 @@
 
         return zc, zw, yc, yw, x_copy, x_wait
 
-    azc, azw, ayc, ayw, axc, axw = gather(win, az_s, az_r, ay_s, ay_r, ax_s, ax_r)
+    def zback_z(k):
+        return lax.rem(z + zs - k, zs)
+
+    def azc(k):
+        return rcopy(win.at[z, gh], win.at[z, gh], az_s.at[k], az_r.at[k], zfwd(k))
+
+    def azw(k):
+        s = win.at[zback_z(k), gh]
+        return rcopy(s, s, az_s.at[k], az_r.at[k], zfwd(k))
+
+    def axc(k):
+        s = win.at[zback_z(k), gh]
+        return rcopy(s, s, ax_s.at[k], ax_r.at[k], xpeer)
+
+    def axw(k):
+        s = win.at[zback_z(k), 1 - gh]
+        return rcopy(s, s, ax_s.at[k], ax_r.at[k], xpeer)
+
     bzc, bzw, byc, byw, bxc, bxw = gather(wo, bz_s, bz_r, by_s, by_r, bx_s, bx_r)
 
     lc_in[0].wait()
     lc_in[1].wait()
     loop(1, zs, lambda k: azc(k).start())
-    ayc(0).start()
 
     e_up = rcopy(up_hbm.at[0], up.at[c], es.at[0], er.at[0], cpeer)
     e_down = rcopy(down_hbm.at[0], down.at[c], es.at[1], er.at[1], cpeer)
@@ -132,57 +148,61 @@
 
     lc_tok.wait()
     step_rows = 32
-    rin = nb.shape[2]
+    rin = nb.shape[4]
 
     def norm(i):
         rows = pl.ds(pl.multiple_of(i * step_rows, step_rows), step_rows)
         x = tok[rows, :].astype(F32)
         scale = lax.rsqrt(jnp.mean(x * x, axis=-1, keepdims=True) + 1e-05)
         n = (x * scale * gain_ref[...]).astype(BF16)
+        part = i // (th // step_rows)
+        within = pl.ds(pl.multiple_of(lax.rem(i, th // step_rows) * step_rows, step_rows), step_rows)
         for j in range(wide):
-            nb[j, rows, :] = n[:, j * rin : (j + 1) * rin]
+            nb[j % 2, part, j // 2, within, :] = n[:, j * rin : (j + 1) * rin]
 
     loop(0, tokens // step_rows, norm)
 
-    def madd(b):
-        wb = win[b].reshape(2 * half_in, lcols)
-        acc[...] += jnp.dot(nb[b], wb, preferred_element_type=F32)
+    tsend = rcopy(nb.at[oy, c], nby.at[c], ty_s, ty_r, ypeer)
+    tsend.start()
+    lc_out[0].wait()
+    lc_out[1].wait()
+    byc(0).start()
+
+    def madd(zz):
+        wb = win[zz].reshape(2 * half_in, lcols)
+        for r in range(2):
+            acc[r] += jnp.dot(nb[y, r, zz], wb, preferred_element_type=F32)
+            acc[2 + r] += jnp.dot(nby[r, zz], wb, preferred_element_type=F32)
 
     acc[...] = jnp.zeros_like(acc)
-    madd(w)
 
     def z_arrive(k):
         azw(k).wait_recv()
-        axc(k, False).start()
-        ayc(k).start()
-
-    ayw(0).wait_recv()
-    axc(0, True).start()
+        axc(k).start()
+
     loop(1, zs, z_arrive)
-
-    def y_arrive(k):
-        ayw(k).wait_recv()
-        axc(k, True).start()
-
-    loop(1, zs, y_arrive)
-    lc_out[0].wait()
-    lc_out[1].wait()
     loop(1, zs, lambda k: bzc(k).start())
-
-    def use_far(k):
-        axw(k, True).wait_recv()
-        madd(blk(k, oy))
+    rcopy(nby.at[c], nby.at[c], ty_s, ty_r, ypeer).wait_recv()
+    tfwd = rcopy(nby.at[c], nby.at[c], tc_s, tc_r, cpeer)
+    tfwd.start()
+    rcopy(nby.at[1 - c], nby.at[1 - c], tc_s, tc_r, cpeer).wait_recv()
+    madd(z)
 
     def use_near(k):
-        axw(k, False).wait_recv()
-        madd(blk(k, y))
-
-    use_far(0)
+        axw(k).wait_recv()
+        madd(zback_z(k))
+
     loop(1, zs, use_near)
-    loop(1, zs, use_far)
-
-    lat[w, c] = acc[pl.ds(pl.multiple_of(c * th, th), th), :].astype(BF16)
-    xsend[...] = acc[pl.ds(pl.multiple_of((1 - c) * th, th), th), :].astype(BF16)
+    psend[...] = acc[2:4].astype(BF16)
+    pcopy = rcopy(psend, precv, py_s, py_r, ypeer)
+    pcopy.start()
+    bzw(1).wait_recv()
+    bxc(1, False).start()
+    byc(1).start()
+    pcopy.wait_recv()
+
+    lat[w, c] = (acc[c] + precv[c].astype(F32)).astype(BF16)
+    xsend[...] = (acc[1 - c] + precv[1 - c].astype(F32)).astype(BF16)
     swap = rcopy(xsend, lat.at[w, c], cc_s, cc_r, cpeer)
     swap.start()
     rcopy(xsend, lat.at[w, 1 - c], cc_s, cc_r, cpeer).wait_recv()
@@ -230,7 +250,7 @@
         x = jnp.concatenate([x0, x1], axis=1)
         total = None
         for h in range(2):
-            hid = jnp.dot(x, up[h], preferred_element_type=F32)
+            hid = lax.dot_general(x, up[h], (((1,), (1,)), ((), ())), preferred_element_type=F32)
             hid = jnp.square(jnp.maximum(hid, 0.0)).astype(BF16)
             part = jnp.dot(hid, down[h], preferred_element_type=F32)
             total = part if total is None else total + part
@@ -257,7 +277,7 @@
         bzw(k).wait_recv()
         bxc(k, False).start()
 
-    loop(1, zs, b_arrive)
+    loop(2, zs, b_arrive)
 
     def expert_step(k):
         cyw(k).wait_recv()
@@ -265,6 +285,7 @@
 
         @pl.when(k > 1)
         def _():
+            byc(k).start()
             finish(k - 1)
 
         @pl.when(k == 1)
@@ -273,7 +294,6 @@
             macc[...] = ownp[0] + yrecv[0].astype(F32)
 
     loop(1, zs, expert_step)
-    loop(0, zs, lambda k: byc(k).start())
     finish(zs - 1)
 
     def by_arrive(k):
@@ -312,11 +332,15 @@
     e_down.wait_send()
     swap.wait_send()
     mcopy.wait_send()
-    for zc, yc, xc in ((azc, ayc, axc), (bzc, byc, bxc)):
-        loop(1, zs, lambda k: zc(k).wait_send())
-        loop(0, zs, lambda k: yc(k).wait_send())
-        loop(1, zs, lambda k: xc(k, False).wait_send())
-        loop(0, zs, lambda k: xc(k, True).wait_send())
+    tsend.wait_send()
+    tfwd.wait_send()
+    pcopy.wait_send()
+    loop(1, zs, lambda k: azc(k).wait_send())
+    loop(1, zs, lambda k: axc(k).wait_send())
+    loop(1, zs, lambda k: bzc(k).wait_send())
+    loop(0, zs, lambda k: byc(k).wait_send())
+    loop(1, zs, lambda k: bxc(k, False).wait_send())
+    loop(0, zs, lambda k: bxc(k, True).wait_send())
     loop(1, zs, lambda k: czc(k).wait_send())
     loop(0, zs, lambda k: cyc(k).wait_send())
     loop(0, zs, lambda k: dyc(k).wait_send())
@@ -341,14 +365,17 @@
     V = pltpu.VMEM
     scratch = [
         V((rows, depth), BF16),
-        V((wide, rows, depth // wide), BF16),
-        V((wide, 2, w_in.shape[0] // 2, latent // 2), BF16),
+        V((2, 2, zs, half, depth // wide), BF16),
+        V((2, zs, half, depth // wide), BF16),
+        V((zs, 2, w_in.shape[0] // 2, latent // 2), BF16),
         V((wide, 2, w_out.shape[0] // 2, cols), BF16),
-        V((2, latent, hid), BF16),
+        V((2, hid, latent), BF16),
         V((2, hid, latent), BF16),
         V((wide, wide, half), F32),
         V((wide, 2, half, latent // 2), BF16),
-        V((rows, latent // 2), F32),
+        V((4, half, latent // 2), F32),
+        V((2, half, latent // 2), BF16),
+        V((2, half, latent // 2), BF16),
         V((half, latent // 2), BF16),
         V((2, half, latent), F32),
         V((2, half, latent), F32),
@@ -362,7 +389,7 @@
         dma((wide,)), dma((wide,)),
         dma((2,)), dma((2,)),
     ]
-    scratch += [dma((zs,)), dma((zs,)), dma((zs,)), dma((zs,)), dma((wide,)), dma((wide,))] * 2
+    scratch += [dma((zs,))] * 4 + [dma] * 6 + [dma((zs,))] * 4 + [dma((wide,))] * 2
     scratch += [dma((zs,))] * 4 + [dma, dma] + [dma((zs,))] * 4 + [dma, dma]
     return pl.pallas_call(
         kernel,
@@ -374,7 +401,7 @@
             collective_id=0, has_side_effects=True, vmem_limit_bytes=66_000_000
         ),
         name="moe",
-    )(tokens, norm_gain.reshape(1, depth), w_in, w_out, w_up, w_down, gates)
+    )(tokens, norm_gain.reshape(1, depth), w_in, w_out, w_up.swapaxes(1, 2), w_down, gates)
 
 
 def solution(mesh):

time: 158 us -> 147 us (0.930)
  Pallas kernels: 149 us -> 142 us
  local copies, waits for them, and re-layouts: 6.83 us -> 2.3 us
    pallas_call x1, Pallas kernels: 149 us -> 142 us  [local(): pl.pallas_call(kernel, out_shape=jax.ShapeDtypeStruct((rows, cols), BF16)...]
    unnamed x2 -> x1, local copies, waits for them, and re-layouts: 6.83 us -> 2.3 us
where the time goes in v2:
time: 147 us; the launch traced here: 146 us
  Pallas kernels  142 us (97%)
  local copies, waits for them, and re-layouts  2.3 us (2%)
    pallas_call x1, Pallas kernels, local(): pl.pallas_call(kernel, out_shape=jax.ShapeDtypeStruct((rows, cols), BF16)...  142 us

profile of v2, /device:TPU:20, one launch (start us, length us, event | category | flops | bytes accessed | tf_op | source)
XLA Modules:
  0.0 146.1 jit_solution(4968402241769702606)
XLA Ops:
  0.0 1.3 select_reduce_fusion
  1.3 142.5 %moe.1 = bf16[256,2048]{1,0:T(8,128)(2,1)} custom-call(bf16[256,4096]{1,0:T(8,128)(2,1)} %tok_hbm.1, f32[1,4096]{1,0:T(1,128)} %bitcast.9, bf16[512,1024]{1,0:T(8,128)(2,1)} %win_hbm.1, bf16[128,2048]{1,0:T(8,128)(2,1)} %wout_hbm.1, bf16[1,1344,1024]{2,1,0:T(8,128)(2,1)} %bitcast.7, bf16[1,1344,1024]{2,1,0:T(8,128)(2,1)} %down_hbm.1, f32[2,8,128]{2,1,0:T(8,128)} %bitcast.8), custom_call_target="tpu_custom_call" | custom-call | tf_op jit(solution)/shard_map/moe/pallas_call | solution.py:394
  143.8 2.3 %copy.10 = bf16[256,2048]{1,0:T(8,128)(2,1)} copy(bf16[256,2048]{1,0:T(8,128)(2,1)} %moe.1) | data formatting | bytes 2097152

commit v3 on v2

--- a/solution.py
+++ b/solution.py
@@ -47,8 +47,7 @@
 
         lax.fori_loop(lo, hi, step, 0)
 
-    half_in = win.shape[2]
-    lcols = win.shape[3]
+    pieces, piece, lcols = win.shape[2:]
     half_out = wo.shape[2]
     tokens = tok.shape[0]
     th = lat.shape[2]
@@ -57,9 +56,7 @@
     in_cols = pl.ds(pl.multiple_of(c * lcols, lcols), lcols)
     lc_tok = pltpu.make_async_copy(tok_hbm, tok, loc.at[0])
     lc_in = [
-        pltpu.make_async_copy(
-            win_hbm.at[pl.ds(h * half_in, half_in), in_cols], win.at[z, h], loc.at[1 + h]
-        )
+        pltpu.make_async_copy(win_hbm.at[h, :, :, in_cols], win.at[z, h], loc.at[1 + h])
         for h in range(2)
     ]
     lc_out = [
@@ -110,26 +107,34 @@
     def zback_z(k):
         return lax.rem(z + zs - k, zs)
 
-    def azc(k):
-        return rcopy(win.at[z, gh], win.at[z, gh], az_s.at[k], az_r.at[k], zfwd(k))
-
-    def azw(k):
-        s = win.at[zback_z(k), gh]
-        return rcopy(s, s, az_s.at[k], az_r.at[k], zfwd(k))
-
-    def axc(k):
-        s = win.at[zback_z(k), gh]
-        return rcopy(s, s, ax_s.at[k], ax_r.at[k], xpeer)
-
-    def axw(k):
-        s = win.at[zback_z(k), 1 - gh]
-        return rcopy(s, s, ax_s.at[k], ax_r.at[k], xpeer)
+    def azc(k, q):
+        i = q * zs + k
+        return rcopy(win.at[z, gh, q], win.at[z, gh, q], az_s.at[i], az_r.at[i], zfwd(k))
+
+    def azw(k, q):
+        s = win.at[zback_z(k), gh, q]
+        i = q * zs + k
+        return rcopy(s, s, az_s.at[i], az_r.at[i], zfwd(k))
+
+    def axc(k, q):
+        s = win.at[zback_z(k), gh, q]
+        i = q * zs + k
+        return rcopy(s, s, ax_s.at[i], ax_r.at[i], xpeer)
+
+    def axw(k, q):
+        s = win.at[zback_z(k), 1 - gh, q]
+        i = q * zs + k
+        return rcopy(s, s, ax_s.at[i], ax_r.at[i], xpeer)
+
+    def each_piece(body):
+        for q in range(pieces):
+            loop(1, zs, lambda k: body(k, q))
 
     bzc, bzw, byc, byw, bxc, bxw = gather(wo, bz_s, bz_r, by_s, by_r, bx_s, bx_r)
 
     lc_in[0].wait()
     lc_in[1].wait()
-    loop(1, zs, lambda k: azc(k).start())
+    each_piece(lambda k, q: azc(k, q).start())
 
     e_up = rcopy(up_hbm.at[0], up.at[c], es.at[0], er.at[0], cpeer)
     e_down = rcopy(down_hbm.at[0], down.at[c], es.at[1], er.at[1], cpeer)
@@ -169,19 +174,19 @@
     byc(0).start()
 
     def madd(zz):
-        wb = win[zz].reshape(2 * half_in, lcols)
+        wb = win[zz].reshape(2 * pieces * piece, lcols)
         for r in range(2):
             acc[r] += jnp.dot(nb[y, r, zz], wb, preferred_element_type=F32)
             acc[2 + r] += jnp.dot(nby[r, zz], wb, preferred_element_type=F32)
 
     acc[...] = jnp.zeros_like(acc)
 
-    def z_arrive(k):
-        azw(k).wait_recv()
-        axc(k).start()
-
-    loop(1, zs, z_arrive)
-    loop(1, zs, lambda k: bzc(k).start())
+    def z_arrive(k, q):
+        azw(k, q).wait_recv()
+        axc(k, q).start()
+
+    each_piece(z_arrive)
+    loop(1, zs - 1, lambda k: bzc(k).start())
     rcopy(nby.at[c], nby.at[c], ty_s, ty_r, ypeer).wait_recv()
     tfwd = rcopy(nby.at[c], nby.at[c], tc_s, tc_r, cpeer)
     tfwd.start()
@@ -189,7 +194,8 @@
     madd(z)
 
     def use_near(k):
-        axw(k).wait_recv()
+        for q in range(pieces):
+            axw(k, q).wait_recv()
         madd(zback_z(k))
 
     loop(1, zs, use_near)
@@ -201,29 +207,43 @@
     byc(1).start()
     pcopy.wait_recv()
 
-    lat[w, c] = (acc[c] + precv[c].astype(F32)).astype(BF16)
+    hrow = th // 2
+
+    def lpiece(b, q, r):
+        return lat.at[b, q, pl.ds(r * hrow, hrow)]
+
+    def czc(k, q, r):
+        s = lpiece(w, q, r)
+        i = (q * 2 + r) * zs + k
+        return rcopy(s, s, cz_s.at[i], cz_r.at[i], zfwd(k))
+
+    def czw(k, q, r):
+        s = lpiece(blk(k, y), q, r)
+        i = (q * 2 + r) * zs + k
+        return rcopy(s, s, cz_s.at[i], cz_r.at[i], zfwd(k))
+
+    def cyc(k, q, r):
+        s = lpiece(blk(k, y), q, r)
+        i = (q * 2 + r) * zs + k
+        return rcopy(s, s, cy_s.at[i], cy_r.at[i], ypeer)
+
+    def cyw(k, q, r):
+        s = lpiece(blk(k, oy), q, r)
+        i = (q * 2 + r) * zs + k
+        return rcopy(s, s, cy_s.at[i], cy_r.at[i], ypeer)
+
     xsend[...] = (acc[1 - c] + precv[1 - c].astype(F32)).astype(BF16)
     swap = rcopy(xsend, lat.at[w, c], cc_s, cc_r, cpeer)
     swap.start()
+    lat[w, c] = (acc[c] + precv[c].astype(F32)).astype(BF16)
+    for r in range(2):
+        cyc(0, c, r).start()
+        loop(1, zs, lambda k: czc(k, c, r).start())
     rcopy(xsend, lat.at[w, 1 - c], cc_s, cc_r, cpeer).wait_recv()
-
-    def czc(k):
-        return rcopy(lat.at[w], lat.at[w], cz_s.at[k], cz_r.at[k], zfwd(k))
-
-    def czw(k):
-        s = lat.at[blk(k, y)]
-        return rcopy(s, s, cz_s.at[k], cz_r.at[k], zfwd(k))
-
-    def cyc(k):
-        s = lat.at[blk(k, y)]
-        return rcopy(s, s, cy_s.at[k], cy_r.at[k], ypeer)
-
-    def cyw(k):
-        s = lat.at[blk(k, oy)]
-        return rcopy(s, s, cy_s.at[k], cy_r.at[k], ypeer)
-
-    cyc(0).start()
-    loop(1, zs, lambda k: czc(k).start())
+    for r in range(2):
+        cyc(0, 1 - c, r).start()
+        loop(1, zs, lambda k: czc(k, 1 - c, r).start())
+    loop(zs - 1, zs, lambda k: bzc(k).start())
 
     lc_up.wait()
     lc_down.wait()
@@ -265,12 +285,20 @@
         zsend[k] = (ownp[lax.rem(k, 2)] + yrecv[k].astype(F32)).astype(BF16)
         dzc(k).start()
 
-    def arrive(k):
-        czw(k).wait_recv()
-        cyc(k).start()
-
-    loop(1, zs, arrive)
-    cyw(0).wait_recv()
+    order = [(q, r) for q in (c, 1 - c) for r in range(2)]
+
+    def arrive(k, q, r):
+        czw(k, q, r).wait_recv()
+        cyc(k, q, r).start()
+
+    for q, r in order:
+        loop(1, zs, lambda k: arrive(k, q, r))
+
+    def far_rows(k):
+        for q, r in order:
+            cyw(k, q, r).wait_recv()
+
+    far_rows(0)
     expert(0)
 
     def b_arrive(k):
@@ -280,7 +308,7 @@
     loop(2, zs, b_arrive)
 
     def expert_step(k):
-        cyw(k).wait_recv()
+        far_rows(k)
         expert(k)
 
         @pl.when(k > 1)
@@ -335,14 +363,15 @@
     tsend.wait_send()
     tfwd.wait_send()
     pcopy.wait_send()
-    loop(1, zs, lambda k: azc(k).wait_send())
-    loop(1, zs, lambda k: axc(k).wait_send())
+    each_piece(lambda k, q: azc(k, q).wait_send())
+    each_piece(lambda k, q: axc(k, q).wait_send())
     loop(1, zs, lambda k: bzc(k).wait_send())
     loop(0, zs, lambda k: byc(k).wait_send())
     loop(1, zs, lambda k: bxc(k, False).wait_send())
     loop(0, zs, lambda k: bxc(k, True).wait_send())
-    loop(1, zs, lambda k: czc(k).wait_send())
-    loop(0, zs, lambda k: cyc(k).wait_send())
+    for q, r in order:
+        loop(1, zs, lambda k: czc(k, q, r).wait_send())
+        loop(0, zs, lambda k: cyc(k, q, r).wait_send())
     loop(0, zs, lambda k: dyc(k).wait_send())
     loop(1, zs, lambda k: dzc(k).wait_send())
 
@@ -353,6 +382,8 @@
     rows, depth = tokens.shape
     half = rows // 2
     latent = w_in.shape[1]
+    pieces = 4
+    piece = w_in.shape[0] // (2 * pieces)
     ids = expert_ids.T
     chosen = ids[:, None, :] == jnp.arange(wide, dtype=jnp.int32)[None, :, None]
     gates = jnp.sum(jnp.where(chosen, gate_weights.T[:, None, :], 0.0), axis=0)
@@ -367,7 +398,7 @@
         V((rows, depth), BF16),
         V((2, 2, zs, half, depth // wide), BF16),
         V((2, zs, half, depth // wide), BF16),
-        V((zs, 2, w_in.shape[0] // 2, latent // 2), BF16),
+        V((zs, 2, pieces, piece, latent // 2), BF16),
         V((wide, 2, w_out.shape[0] // 2, cols), BF16),
         V((2, hid, latent), BF16),
         V((2, hid, latent), BF16),
@@ -389,8 +420,8 @@
         dma((wide,)), dma((wide,)),
         dma((2,)), dma((2,)),
     ]
-    scratch += [dma((zs,))] * 4 + [dma] * 6 + [dma((zs,))] * 4 + [dma((wide,))] * 2
-    scratch += [dma((zs,))] * 4 + [dma, dma] + [dma((zs,))] * 4 + [dma, dma]
+    scratch += [dma((pieces * zs,))] * 4 + [dma] * 6 + [dma((zs,))] * 4 + [dma((wide,))] * 2
+    scratch += [dma((4 * zs,))] * 4 + [dma, dma] + [dma((zs,))] * 4 + [dma, dma]
     return pl.pallas_call(
         kernel,
         out_shape=jax.ShapeDtypeStruct((rows, cols), BF16),
@@ -401,7 +432,7 @@
             collective_id=0, has_side_effects=True, vmem_limit_bytes=66_000_000
         ),
         name="moe",
-    )(tokens, norm_gain.reshape(1, depth), w_in, w_out, w_up.swapaxes(1, 2), w_down, gates)
+    )(tokens, norm_gain.reshape(1, depth), w_in.reshape(2, pieces, piece, latent), w_out, w_up.swapaxes(1, 2), w_down, gates)
 
 
 def solution(mesh):

time: 147 us -> 143 us (0.973)
  Pallas kernels: 142 us -> 139 us
    pallas_call x1, Pallas kernels: 142 us -> 139 us  [local(): pl.pallas_call(kernel, out_shape=jax.ShapeDtypeStruct((rows, cols), BF16)...]
where the time goes in v3:
time: 143 us; the launch traced here: 142 us
  Pallas kernels  139 us (97%)
  local copies, waits for them, and re-layouts  2.3 us (2%)
    pallas_call x1, Pallas kernels, local(): pl.pallas_call(kernel, out_shape=jax.ShapeDtypeStruct((rows, cols), BF16)...  139 us

profile of v3, /device:TPU:20, one launch (start us, length us, event | category | flops | bytes accessed | tf_op | source)
XLA Modules:
  0.0 142.3 jit_solution(12919449019088718303)
XLA Ops:
  0.0 1.3 select_reduce_fusion
  1.3 138.7 %moe.1 = bf16[256,2048]{1,0:T(8,128)(2,1)} custom-call(bf16[256,4096]{1,0:T(8,128)(2,1)} %tok_hbm.1, f32[1,4096]{1,0:T(1,128)} %bitcast.11, bf16[2,4,64,1024]{3,2,1,0:T(8,128)(2,1)} %bitcast.9, bf16[128,2048]{1,0:T(8,128)(2,1)} %wout_hbm.1, bf16[1,1344,1024]{2,1,0:T(8,128)(2,1)} %bitcast.8, bf16[1,1344,1024]{2,1,0:T(8,128)(2,1)} %down_hbm.1, ...), custom_call_target="tpu_custom_call" | custom-call | tf_op jit(solution)/shard_map/moe/pallas_call | solution.py:425
  140.0 2.3 %copy.10 = bf16[256,2048]{1,0:T(8,128)(2,1)} copy(bf16[256,2048]{1,0:T(8,128)(2,1)} %moe.1) | data formatting | bytes 2097152

commit v4 on v3

--- a/solution.py
+++ b/solution.py
@@ -238,11 +238,18 @@
     lat[w, c] = (acc[c] + precv[c].astype(F32)).astype(BF16)
     for r in range(2):
         cyc(0, c, r).start()
-        loop(1, zs, lambda k: czc(k, c, r).start())
+        czc(1, c, r).start()
     rcopy(xsend, lat.at[w, 1 - c], cc_s, cc_r, cpeer).wait_recv()
     for r in range(2):
         cyc(0, 1 - c, r).start()
-        loop(1, zs, lambda k: czc(k, 1 - c, r).start())
+        czc(1, 1 - c, r).start()
+
+    def later(k):
+        for q in (c, 1 - c):
+            for r in range(2):
+                czc(k, q, r).start()
+
+    loop(2, zs, later)
     loop(zs - 1, zs, lambda k: bzc(k).start())
 
     lc_up.wait()
@@ -257,11 +264,15 @@
         row = jnp.sum(jnp.where(mine, gt, 0.0), axis=0, keepdims=True)
         return jnp.transpose(jnp.broadcast_to(row, (8, th)))[:, :1]
 
-    def dyc(k):
-        return rcopy(ysend.at[k], yrecv.at[k], dy_s.at[k], dy_r.at[k], ypeer)
-
-    def dzc(k):
-        return rcopy(zsend.at[k], zrecv.at[k], dz_s.at[k], dz_r.at[k], zback(k))
+    hcol = ysend.shape[3]
+
+    def dyc(k, q):
+        i = q * zs + k
+        return rcopy(ysend.at[k, q], yrecv.at[k, q], dy_s.at[i], dy_r.at[i], ypeer)
+
+    def dzc(k, q):
+        i = q * zs + k
+        return rcopy(zsend.at[k, q], zrecv.at[k, q], dz_s.at[i], dz_r.at[i], zback(k))
 
     def expert(k):
         b0 = blk(k, 0)
@@ -276,14 +287,17 @@
             total = part if total is None else total + part
         obuf[0] = total[:th] * gate_col(b0)
         obuf[1] = total[th:] * gate_col(b0 + 1)
-        ysend[k] = obuf[oy].astype(BF16)
-        dyc(k).start()
+        for q in range(2):
+            ysend[k, q] = obuf[oy, :, q * hcol : (q + 1) * hcol].astype(BF16)
+            dyc(k, q).start()
         ownp[lax.rem(k, 2)] = obuf[y]
 
     def finish(k):
-        dyc(k).wait_recv()
-        zsend[k] = (ownp[lax.rem(k, 2)] + yrecv[k].astype(F32)).astype(BF16)
-        dzc(k).start()
+        for q in range(2):
+            dyc(k, q).wait_recv()
+            own = ownp[lax.rem(k, 2), :, q * hcol : (q + 1) * hcol]
+            zsend[k, q] = (own + yrecv[k, q].astype(F32)).astype(BF16)
+            dzc(k, q).start()
 
     order = [(q, r) for q in (c, 1 - c) for r in range(2)]
 
@@ -291,48 +305,61 @@
         czw(k, q, r).wait_recv()
         cyc(k, q, r).start()
 
-    for q, r in order:
-        loop(1, zs, lambda k: arrive(k, q, r))
+    def arrive_all(k):
+        for q, r in order:
+            arrive(k, q, r)
 
     def far_rows(k):
         for q, r in order:
             cyw(k, q, r).wait_recv()
 
-    far_rows(0)
-    expert(0)
-
     def b_arrive(k):
         bzw(k).wait_recv()
         bxc(k, False).start()
-
-    loop(2, zs, b_arrive)
-
-    def expert_step(k):
-        far_rows(k)
-        expert(k)
-
-        @pl.when(k > 1)
-        def _():
-            byc(k).start()
-            finish(k - 1)
-
-        @pl.when(k == 1)
-        def _():
-            dyc(0).wait_recv()
-            macc[...] = ownp[0] + yrecv[0].astype(F32)
-
-    loop(1, zs, expert_step)
-    finish(zs - 1)
+        byc(k).start()
 
     def by_arrive(k):
         byw(k).wait_recv()
         bxc(k, True).start()
 
-    loop(0, zs, by_arrive)
+    arrive_all(1)
+    far_rows(0)
+    expert(0)
+    by_arrive(0)
+
+    def expert_step(k):
+        @pl.when(k < zs - 1)
+        def _():
+            arrive_all(k + 1)
+
+        far_rows(k)
+        expert(k)
+
+        @pl.when(k > 1)
+        def _():
+            finish(k - 1)
+
+        @pl.when(k == 1)
+        def _():
+            for q in range(2):
+                dyc(0, q).wait_recv()
+                cols = slice(q * hcol, (q + 1) * hcol)
+                macc[:, cols] = ownp[0, :, cols] + yrecv[0, q].astype(F32)
+            by_arrive(1)
+
+        @pl.when((k > 1) & (k < zs - 1))
+        def _():
+            b_arrive(k)
+
+    loop(1, zs, expert_step)
+    loop(zs - 1, zs, b_arrive)
+    finish(zs - 1)
+    loop(2, zs, by_arrive)
 
     def collect(k):
-        dzc(k).wait_recv()
-        macc[...] += zrecv[k].astype(F32)
+        for q in range(2):
+            dzc(k, q).wait_recv()
+            macc[:, q * hcol : (q + 1) * hcol] += zrecv[k, q].astype(F32)
 
     loop(1, zs, collect)
     mixb[c] = macc[...].astype(BF16)
@@ -372,8 +399,9 @@
     for q, r in order:
         loop(1, zs, lambda k: czc(k, q, r).wait_send())
         loop(0, zs, lambda k: cyc(k, q, r).wait_send())
-    loop(0, zs, lambda k: dyc(k).wait_send())
-    loop(1, zs, lambda k: dzc(k).wait_send())
+    for q in range(2):
+        loop(0, zs, lambda k: dyc(k, q).wait_send())
+        loop(1, zs, lambda k: dzc(k, q).wait_send())
 
 
 def local(tokens, norm_gain, w_in, w_out, w_up, w_down, expert_ids, gate_weights):
@@ -410,10 +438,10 @@
         V((half, latent // 2), BF16),
         V((2, half, latent), F32),
         V((2, half, latent), F32),
-        V((zs, half, latent), BF16),
-        V((zs, half, latent), BF16),
-        V((zs, half, latent), BF16),
-        V((zs, half, latent), BF16),
+        V((zs, 2, half, latent // 2), BF16),
+        V((zs, 2, half, latent // 2), BF16),
+        V((zs, 2, half, latent // 2), BF16),
+        V((zs, 2, half, latent // 2), BF16),
         V((half, latent), F32),
         V((2, half, latent), BF16),
         dma((8,)),
@@ -421,7 +449,7 @@
         dma((2,)), dma((2,)),
     ]
     scratch += [dma((pieces * zs,))] * 4 + [dma] * 6 + [dma((zs,))] * 4 + [dma((wide,))] * 2
-    scratch += [dma((4 * zs,))] * 4 + [dma, dma] + [dma((zs,))] * 4 + [dma, dma]
+    scratch += [dma((4 * zs,))] * 4 + [dma, dma] + [dma((2 * zs,))] * 4 + [dma, dma]
     return pl.pallas_call(
         kernel,
         out_shape=jax.ShapeDtypeStruct((rows, cols), BF16),

time: 143 us -> 135 us (0.944)
  Pallas kernels: 139 us -> 131 us
    pallas_call x1, Pallas kernels: 139 us -> 131 us  [local(): pl.pallas_call(kernel, out_shape=jax.ShapeDtypeStruct((rows, cols), BF16)...]
where the time goes in v4:
time: 135 us
  Pallas kernels  131 us (97%)
  local copies, waits for them, and re-layouts  2.3 us (2%)
    pallas_call x1, Pallas kernels, local(): pl.pallas_call(kernel, out_shape=jax.ShapeDtypeStruct((rows, cols), BF16)...  131 us

profile of v4, /device:TPU:20, one launch (start us, length us, event | category | flops | bytes accessed | tf_op | source)
XLA Modules:
  0.0 135.0 jit_solution(14121118175776952861)
XLA Ops:
  0.0 1.3 select_reduce_fusion
  1.3 131.4 %moe.1 = bf16[256,2048]{1,0:T(8,128)(2,1)} custom-call(bf16[256,4096]{1,0:T(8,128)(2,1)} %tok_hbm.1, f32[1,4096]{1,0:T(1,128)} %bitcast.11, bf16[2,4,64,1024]{3,2,1,0:T(8,128)(2,1)} %bitcast.9, bf16[128,2048]{1,0:T(8,128)(2,1)} %wout_hbm.1, bf16[1,1344,1024]{2,1,0:T(8,128)(2,1)} %bitcast.8, bf16[1,1344,1024]{2,1,0:T(8,128)(2,1)} %down_hbm.1, ...), custom_call_target="tpu_custom_call" | custom-call | tf_op jit(solution)/shard_map/moe/pallas_call | solution.py:453
  132.7 2.3 %copy.10 = bf16[256,2048]{1,0:T(8,128)(2,1)} copy(bf16[256,2048]{1,0:T(8,128)(2,1)} %moe.1) | data formatting | bytes 2097152

commit v5 on v4

--- a/solution.py
+++ b/solution.py
@@ -135,6 +135,10 @@
     lc_in[0].wait()
     lc_in[1].wait()
     each_piece(lambda k, q: azc(k, q).start())
+    lc_out[0].wait()
+    lc_out[1].wait()
+    byc(0).start()
+    loop(1, zs, lambda k: bzc(k).start())
 
     e_up = rcopy(up_hbm.at[0], up.at[c], es.at[0], er.at[0], cpeer)
     e_down = rcopy(down_hbm.at[0], down.at[c], es.at[1], er.at[1], cpeer)
@@ -169,9 +173,6 @@
 
     tsend = rcopy(nb.at[oy, c], nby.at[c], ty_s, ty_r, ypeer)
     tsend.start()
-    lc_out[0].wait()
-    lc_out[1].wait()
-    byc(0).start()
 
     def madd(zz):
         wb = win[zz].reshape(2 * pieces * piece, lcols)
@@ -186,7 +187,6 @@
         axc(k, q).start()
 
     each_piece(z_arrive)
-    loop(1, zs - 1, lambda k: bzc(k).start())
     rcopy(nby.at[c], nby.at[c], ty_s, ty_r, ypeer).wait_recv()
     tfwd = rcopy(nby.at[c], nby.at[c], tc_s, tc_r, cpeer)
     tfwd.start()
@@ -198,13 +198,13 @@
             axw(k, q).wait_recv()
         madd(zback_z(k))
 
+    bzw(1).wait_recv()
+    bxc(1, False).start()
+    byc(1).start()
     loop(1, zs, use_near)
     psend[...] = acc[2:4].astype(BF16)
     pcopy = rcopy(psend, precv, py_s, py_r, ypeer)
     pcopy.start()
-    bzw(1).wait_recv()
-    bxc(1, False).start()
-    byc(1).start()
     pcopy.wait_recv()
 
     hrow = th // 2
@@ -250,7 +250,6 @@
                 czc(k, q, r).start()
 
     loop(2, zs, later)
-    loop(zs - 1, zs, lambda k: bzc(k).start())
 
     lc_up.wait()
     lc_down.wait()

time: 135 us -> 139 us (1.030)
  Pallas kernels: 131 us -> 135 us
    pallas_call x1, Pallas kernels: 131 us -> 135 us  [local(): pl.pallas_call(kernel, out_shape=jax.ShapeDtypeStruct((rows, cols), BF16)...]
where the time goes in v5:
time: 139 us
  Pallas kernels  135 us (97%)
  local copies, waits for them, and re-layouts  2.3 us (2%)
    pallas_call x1, Pallas kernels, local(): pl.pallas_call(kernel, out_shape=jax.ShapeDtypeStruct((rows, cols), BF16)...  135 us

profile of v5, /device:TPU:20, one launch (start us, length us, event | category | flops | bytes accessed | tf_op | source)
XLA Modules:
  0.0 139.0 jit_solution(10444318562316086785)
XLA Ops:
  0.0 1.3 select_reduce_fusion
  1.3 135.4 %moe.1 = bf16[256,2048]{1,0:T(8,128)(2,1)} custom-call(bf16[256,4096]{1,0:T(8,128)(2,1)} %tok_hbm.1, f32[1,4096]{1,0:T(1,128)} %bitcast.11, bf16[2,4,64,1024]{3,2,1,0:T(8,128)(2,1)} %bitcast.9, bf16[128,2048]{1,0:T(8,128)(2,1)} %wout_hbm.1, bf16[1,1344,1024]{2,1,0:T(8,128)(2,1)} %bitcast.8, bf16[1,1344,1024]{2,1,0:T(8,128)(2,1)} %down_hbm.1, ...), custom_call_target="tpu_custom_call" | custom-call | tf_op jit(solution)/shard_map/moe/pallas_call | solution.py:452
  136.7 2.3 %copy.10 = bf16[256,2048]{1,0:T(8,128)(2,1)} copy(bf16[256,2048]{1,0:T(8,128)(2,1)} %moe.1) | data formatting | bytes 2097152
